TPU v7x, 32 devices: a whole 2x2x4 slice. The times are simulated.
32 devices in a mesh: gx: 8 (over y, x, core), gy: 4 (over z).
Axes of the slice: x: 2, y: 2, z: 4, core: 2. Of those that a mesh axis runs over, the one named last changes fastest.
Arguments:
- features: bfloat16 [16384, 128], P(('gx', 'gy')), may hold values from -6 to 6
- cache_in: bfloat16 [16384, 128], replicated, may hold values from -26 to 26
- cache_hidden: bfloat16 [16384, 128], replicated, may hold values from -26 to 26
- tiles: bfloat16 [32, 32, 256, 256], P(('gx', 'gy')), may hold values from -0.0625 to 0.0625
- tile_pos: int32 [32, 32, 2], P(('gx', 'gy')), may hold values from 0 to 1
- order: int32 [2, 32], replicated, may hold values from 0 to 31, each once within a row
- skip: int32 [2, 32], replicated, may hold values 0 or 1
- w_first: bfloat16 [128, 128], replicated, may hold values from -0.5 to 0.5
- w_second: bfloat16 [128, 128], replicated, may hold values from -0.5 to 0.5
Outputs:
- output: bfloat16 [16384, 128], P(('gx', 'gy'))
- drift: float32 [2], replicated
Inputs may be any that keep to these rules, and one draw needn't show every extreme that they name: `order`: each row names every block once.
All inputs are finite; a program needn't handle non-finite values.
Results may differ from a plain program's by a relative error of at most 0.0052.
Values may be sent and summed in bfloat16 or wider, within the bound.
A program may use at most 192 MiB of HBM per device.

v0:
```python
import jax
import jax.numpy as jnp
from jax import lax
from jax.sharding import PartitionSpec as P


def refreshed_flags(order, skip):
    block_count = order.shape[1]
    round_hits = (
        order[:, :, None] == jnp.arange(block_count, dtype=jnp.int32)[None, None, :]
    ).astype(jnp.int32)
    return jnp.sum(round_hits * (1 - skip)[:, :, None], axis=1)


def make_fold(cached, fresh_flags, my_tiles, my_pos, own_index):
    tile_rows = my_tiles.shape[1]
    block_rows = 2 * tile_rows

    def fold_step(carry, piece, start):
        piece_blocks = piece.shape[0] // block_rows
        feat_width = piece.shape[1]
        new_blocks = piece.reshape(piece_blocks, 2, tile_rows, feat_width)
        old_blocks = cached.reshape(piece_blocks, 2, tile_rows, feat_width)
        block_ids = jnp.arange(piece_blocks, dtype=jnp.int32)
        use_new = (fresh_flags == 1) | (block_ids == own_index)
        source = jnp.where(use_new[:, None, None, None], new_blocks, old_blocks)
        halves = jnp.where((my_pos[:, 1] == 0)[:, None, None], source[:, 0], source[:, 1])
        products = jnp.einsum("kab,kbf->kaf", my_tiles, halves, preferred_element_type=jnp.float32)
        upper = (my_pos[:, 0] == 0)[:, None, None]
        upper_sum = jnp.sum(jnp.where(upper, products, jnp.float32(0.0)), axis=0)
        lower_sum = jnp.sum(jnp.where(upper, jnp.float32(0.0), products), axis=0)
        summed = jnp.concatenate([upper_sum, lower_sum], axis=0)
        drift_sum = carry[1]
        return (summed, drift_sum)

    return fold_step


def aggregate(block, cached, fresh_flags, my_tiles, my_pos, own_index):
    initial = (jnp.zeros(block.shape, jnp.float32), jnp.zeros((), jnp.float32))
    fold_step = make_fold(cached, fresh_flags, my_tiles, my_pos, own_index)
    column = lax.all_gather(block, "gy", axis=0, tiled=True)
    return fold_step(initial, lax.all_gather(column, "gx", axis=0, tiled=True), jnp.int32(0))


def owner_terms(block, cached, own_index):
    block_rows = block.shape[0]
    own_cache = lax.dynamic_slice_in_dim(cached, own_index * block_rows, block_rows, 0)
    change = block.astype(jnp.float32) - own_cache.astype(jnp.float32)
    return jnp.sum(change * change)


def drift_total(block, cached, own_index):
    return lax.psum(owner_terms(block, cached, own_index), ("gx", "gy"))


def on_device(features, cache_in, cache_hidden, tiles, tile_pos, order, skip, w_first, w_second):
    own_index = lax.axis_index(("gx", "gy"))
    fresh_flags = refreshed_flags(order, skip)
    my_tiles = tiles[0]
    my_pos = tile_pos[0]
    input_cells = cache_in.shape[0] * cache_in.shape[1]
    hidden_cells = cache_hidden.shape[0] * cache_hidden.shape[1]
    drift_input = drift_total(features, cache_in, own_index)
    first_sum, fold_first = aggregate(
        features, cache_in, fresh_flags[0], my_tiles, my_pos, own_index
    )
    first_agg = first_sum.astype(jnp.bfloat16)
    hidden = jnp.maximum(
        jnp.dot(first_agg, w_first, preferred_element_type=jnp.float32), 0.0
    ).astype(jnp.bfloat16)
    drift_hidden = drift_total(hidden, cache_hidden, own_index)
    second_sum, fold_second = aggregate(
        hidden, cache_hidden, fresh_flags[1], my_tiles, my_pos, own_index
    )
    output = jnp.dot(
        second_sum.astype(jnp.bfloat16), w_second, preferred_element_type=jnp.float32
    ).astype(jnp.bfloat16)
    drift = jnp.stack([drift_input / input_cells, drift_hidden / hidden_cells])
    return (output, drift)


def solution(mesh):
    in_specs = (
        P(("gx", "gy"), None),
        P(),
        P(),
        P(("gx", "gy"), None, None, None),
        P(("gx", "gy"), None, None),
        P(),
        P(),
        P(),
        P(),
    )
    out_specs = (P(("gx", "gy"), None), P())
    return jax.shard_map(
        on_device, mesh=mesh, in_specs=in_specs, out_specs=out_specs, check_vma=False
    )
```

profile of v0, /device:TPU:0, one launch (start us, length us, event | category | flops | bytes accessed | tf_op | source)
XLA Modules:
  0.0 164.2 jit_solution(9931714498727391533)
XLA Ops:
  7.2 0.0 copy-start
  7.2 0.0 all-gather.3.cloned.1.call-start
  7.2 19.3 %all_gather.12 = bf16[2048,128]{1,0:T(8,128)(2,1)} all-gather(bf16[512,128]{1,0:T(8,128)(2,1)} %param.9), channel_id=1, replica_groups=mesh['gx'=8,'gy'=4] {'gy'}, dimensions={0}, use_global_device_ids=true | all-gather | bytes 655360 | tf_op jit(solution)/shard_map/all_gather | solution.py:42
  26.6 0.0 all-gather.3.cloned.1.call-update
  26.6 0.0 all-gather.5.cloned.1.call-start
  26.6 0.0 copy-start.4
  26.7 0.0 copy-start.3
  26.7 0.0 copy-start.5
  26.7 6.4 %copy.16 = bf16[32,2,256,128]{2,3,0,1:T(8,128)(2,1)} copy(bf16[32,2,256,128]{3,2,1,0:T(8,128)(2,1)} %bitcast.66) | data formatting | bytes 8388608 | tf_op jit(solution)/shard_map/reshape | solution.py:23
  33.1 0.0 copy-done.4
  33.1 0.0 copy-done.3
  33.1 0.1 select_reduce_fusion.4
  33.2 0.0 copy-done.5
  33.2 29.9 %all-gather.3.cloned.1.call-done = bf16[16384,128]{1,0:T(8,128)(2,1)} async-done(((bf16[2048,128]{1,0:T(8,128)(2,1)}), bf16[16384,128]{1,0:T(8,128)(2,1)}) %all-gather.3.cloned.1.call-update) | async-done | bytes 4194320 | tf_op jit(solution)/shard_map/all_gather | solution.py:43
  63.1 6.4 %copy.15 = bf16[32,2,256,128]{2,3,0,1:T(8,128)(2,1)} copy(bf16[32,2,256,128]{3,2,1,0:T(8,128)(2,1)} %bitcast.68) | data formatting | bytes 8388608 | tf_op jit(solution)/shard_map/reshape | solution.py:22
  69.4 0.0 copy-start.6
  69.4 4.1 %broadcast_select_fusion = bf16[32,2,256,128]{2,3,0,1:T(8,128)(2,1)S(1)} fusion(bf16[32,2,256,128]{2,3,0,1:T(8,128)(2,1)} %copy.15, bf16[32,2,256,128]{2,3,0,1:T(8,128)(2,1)} %copy.16, pred[32]{0:T(512)(128)(4,1)S(1)} %get-tuple-element.9), kind=kLoop, calls=%fused_computation.8 | loop fusion | flops 2097152 | bytes 12582944 | tf_op jit(solution)/shard_map/jit(_where)/select_n | solution.py:26
  73.6 0.5 copy-done.6
  74.1 1.6 select_reduce_fusion.3
  75.7 0.0 copy-done
  75.7 1.8 %multiply_reduce_fusion = (f32[]{:T(128)}, bf16[512,128]{1,0:T(8,128)(2,1)S(1)}) fusion(bf16[16384,128]{1,0:T(8,128)(2,1)} %param.11, s32[]{:T(128)S(6)} %select_n.44, bf16[128,128]{1,0:T(8,128)(2,1)S(1)} %copy-done, bf16[256,128]{0,1:T(8,128)(2,1)S(1)} %bitcast.74, bf16[256,128]{0,1:T(8,128)(2,1)S(1)} %bitcast.73), kind=kOutput, calls=%fused_computation.21 | convolution fusion | flops 17498112 | bytes 425992 | tf_op jit(solution)/shard_map/dot_general | solution.py:70
  77.4 16.4 %all_gather.14 = bf16[2048,128]{1,0:T(8,128)(2,1)} all-gather(bf16[512,128]{1,0:T(8,128)(2,1)S(1)} %get-tuple-element.13), channel_id=1, replica_groups=mesh['gx'=8,'gy'=4] {'gy'}, dimensions={0}, use_global_device_ids=true | all-gather | bytes 655360 | tf_op jit(solution)/shard_map/all_gather | solution.py:42
  93.8 0.0 all-gather.5.cloned.1.call-update
  93.8 0.0 copy-start.1
  93.9 6.4 %copy.18 = bf16[32,2,256,128]{2,3,0,1:T(8,128)(2,1)} copy(bf16[32,2,256,128]{3,2,1,0:T(8,128)(2,1)} %bitcast.67) | data formatting | bytes 8388608 | tf_op jit(solution)/shard_map/reshape | solution.py:23
  100.3 0.0 copy-done.1
  100.3 1.6 multiply_reduce_fusion.1
  101.9 40.2 %all-reduce = (f32[]{:T(128)}, f32[]{:T(128)}) all-reduce(f32[]{:T(128)} %get-tuple-element.12, f32[]{:T(128)} %multiply_reduce_fusion.1), channel_id=1, replica_groups=mesh['gx'=8,'gy'=4] {'gx','gy'}, use_global_device_ids=true, to_apply=%region_8.9 | all-reduce | flops 2 | bytes 16 | tf_op jit(solution)/shard_map/psum | solution.py:54
  143.3 0.6 pad_maximum_fusion
  143.9 0.0 all-gather.5.cloned.1.call-done
  143.9 6.4 %copy.17 = bf16[32,2,256,128]{2,3,0,1:T(8,128)(2,1)} copy(bf16[32,2,256,128]{3,2,1,0:T(8,128)(2,1)} %bitcast.69) | data formatting | bytes 8388608 | tf_op jit(solution)/shard_map/reshape | solution.py:22
  150.3 0.0 copy-start.7
  150.3 4.1 %broadcast_select_fusion.1 = bf16[32,2,256,128]{2,3,0,1:T(8,128)(2,1)S(1)} fusion(bf16[32,2,256,128]{2,3,0,1:T(8,128)(2,1)} %copy.17, bf16[32,2,256,128]{2,3,0,1:T(8,128)(2,1)} %copy.18, pred[32]{0:T(512)(128)(4,1)S(1)} %get-tuple-element.8), kind=kLoop, calls=%fused_computation.9 | loop fusion | flops 2097152 | bytes 12582944 | tf_op jit(solution)/shard_map/jit(_where)/select_n | solution.py:26
  154.4 0.5 copy-done.7
  154.9 0.0 copy-start.2
  154.9 1.6 select_reduce_fusion.1
  156.5 0.0 copy-done.2
  156.5 0.9 convolution_convert_fusion
  (3 shorter events, 0.0 us)
Async XLA Ops:
  7.2 68.5 %copy-start = (bf16[128,128]{1,0:T(8,128)(2,1)S(1)}, bf16[128,128]{1,0:T(8,128)(2,1)}, u32[]{:S(2)}) copy-start(bf16[128,128]{1,0:T(8,128)(2,1)} %param.16) | copy-start | bytes 98308
  7.2 55.9 %all-gather.3.cloned.1.call-start = ((), (), s32[]{:S(2)}) async-start(), calls=%async_computation | async-start | bytes 4718592 | tf_op jit(solution)/shard_map/all_gather | solution.py:43
  26.6 117.3 %all-gather.5.cloned.1.call-start = ((), (), s32[]{:S(2)}) async-start(), calls=%async_computation.1 | async-start | bytes 4718592 | tf_op jit(solution)/shard_map/all_gather | solution.py:43
  26.6 6.4 %copy-start.4 = (s32[2,32]{1,0:T(2,128)S(1)}, s32[2,32]{1,0:T(2,128)}, u32[]{:S(2)}) copy-start(s32[2,32]{1,0:T(2,128)} %param.15) | copy-start | bytes 772
  26.7 6.4 %copy-start.3 = (s32[2,32]{1,0:T(2,128)S(1)}, s32[2,32]{1,0:T(2,128)}, u32[]{:S(2)}) copy-start(s32[2,32]{1,0:T(2,128)} %param.14) | copy-start | bytes 772
  26.7 6.5 %copy-start.5 = (s32[1,32,2]{1,2,0:T(2,128)S(1)}, s32[1,32,2]{1,2,0:T(2,128)}, u32[]{:S(2)}) copy-start(s32[1,32,2]{1,2,0:T(2,128)} %param.13) | copy-start | bytes 772
  69.4 4.6 %copy-start.6 = (bf16[1,32,256,256]{3,2,1,0:T(8,128)(2,1)S(1)}, bf16[1,32,256,256]{3,2,1,0:T(8,128)(2,1)}, u32[]{:S(2)}) copy-start(bf16[1,32,256,256]{3,2,1,0:T(8,128)(2,1)} %param.12) | copy-start | bytes 12582916
  93.8 6.5 %copy-start.1 = (bf16[512,128]{1,0:T(8,128)(2,1)S(1)}, bf16[512,128]{1,0:T(8,128)(2,1)}, u32[]{:S(2)}) copy-start(bf16[512,128]{1,0:T(8,128)(2,1)} %param.9) | copy-start | bytes 393220
  150.3 4.6 %copy-start.7 = (bf16[1,32,256,256]{3,2,1,0:T(8,128)(2,1)S(1)}, bf16[1,32,256,256]{3,2,1,0:T(8,128)(2,1)}, u32[]{:S(2)}) copy-start(bf16[1,32,256,256]{3,2,1,0:T(8,128)(2,1)} %param.12) | copy-start | bytes 12582916
  154.9 1.6 copy-start.2
Sparse Core Ops, SparseCore 0:
  26.7 36.3 all-gather.2
  94.0 37.7 all-gather.4
where the time goes:
time: 165 us; the launch traced here: 164 us
  blocking collectives  75.9 us (46%)
  waiting for transfers between devices  29.9 us (18%)
  local copies, waits for them, and re-layouts  26.6 us (16%)
  between operations  15.5 us (9%)
  other arithmetic  10.5 us (6%)
  matrix products  5.79 us (4%)
    psum x1, blocking collectives, drift_total(): return lax.psum(owner_terms(block, cached, own_index), ('gx', 'gy'))  40.2 us
    all_gather x2, blocking collectives, aggregate(): column = lax.all_gather(block, 'gy', axis=0, tiled=True)  35.7 us
    all_gather x2, waiting for transfers between devices, aggregate(): lax.all_gather(column, 'gx', axis=0, tiled=True)  29.9 us
    reshape x2, local copies, waits for them, and re-layouts, fold_step(): old_blocks = cached.reshape(piece_blocks, 2, tile_rows, feat_width)  12.8 us
    reshape x2, local copies, waits for them, and re-layouts, fold_step(): new_blocks = piece.reshape(piece_blocks, 2, tile_rows, feat_width)  12.7 us
    select_n x2, other arithmetic, fold_step(): source = jnp.where(use_new[:, None, None, None], new_blocks, old_blocks)  8.23 us
  transfers between devices with their start and end apart: 2, of which 1 were waited for; matrix products, arithmetic and copies ran while one was open for 9% of the time, Pallas kernels for 0%

commit v1 on v0

--- a/solution.py
+++ b/solution.py
@@ -51,7 +51,7 @@
 
 
 def drift_total(block, cached, own_index):
-    return lax.psum(owner_terms(block, cached, own_index), ("gx", "gy"))
+    return lax.psum(lax.psum(owner_terms(block, cached, own_index), "gx"), "gy")
 
 
 def on_device(features, cache_in, cache_hidden, tiles, tile_pos, order, skip, w_first, w_second):

time: 165 us -> 152 us (0.921)
  blocking collectives: 75.9 us -> 61.6 us
    psum x1 -> x2, blocking collectives: 40.2 us -> 25.9 us  [drift_total(): return lax.psum(lax.psum(owner_terms(block, cached, own_index), 'gx'), 'gy')]
    all_gather x2, waiting for transfers between devices: 29.9 us -> 31.5 us  [aggregate(): lax.all_gather(column, 'gx', axis=0, tiled=True)]
  transfers between devices with their start and end apart: 2 -> 2, of which waited for: 1 -> 2; matrix products, arithmetic and copies ran while one was open for 9% -> 10% of each run, Pallas kernels for 0% -> 0%
where the time goes in v1:
time: 152 us
  blocking collectives  61.6 us (41%)
  waiting for transfers between devices  31.5 us (21%)
  local copies, waits for them, and re-layouts  26.6 us (18%)
  between operations  15.5 us (10%)
  other arithmetic  10.5 us (7%)
  matrix products  5.79 us (4%)
    all_gather x2, blocking collectives, aggregate(): column = lax.all_gather(block, 'gy', axis=0, tiled=True)  35.7 us
    all_gather x2, waiting for transfers between devices, aggregate(): lax.all_gather(column, 'gx', axis=0, tiled=True)  31.5 us
    psum x2, blocking collectives, drift_total(): return lax.psum(lax.psum(owner_terms(block, cached, own_index), 'gx'), 'gy')  25.9 us
    reshape x2, local copies, waits for them, and re-layouts, fold_step(): old_blocks = cached.reshape(piece_blocks, 2, tile_rows, feat_width)  12.8 us
    reshape x2, local copies, waits for them, and re-layouts, fold_step(): new_blocks = piece.reshape(piece_blocks, 2, tile_rows, feat_width)  12.7 us
    select_n x2, other arithmetic, fold_step(): source = jnp.where(use_new[:, None, None, None], new_blocks, old_blocks)  8.23 us
    dot_general x2, matrix products, fold_step(): jnp.einsum('kab,kbf->kaf', my_tiles, halves, preferred_element_type=jnp.f...  3.15 us
  transfers between devices with their start and end apart: 2, of which 2 were waited for; matrix products, arithmetic and copies ran while one was open for 10% of the time, Pallas kernels for 0%

profile of v1, /device:TPU:0, one launch (start us, length us, event | category | flops | bytes accessed | tf_op | source)
XLA Modules:
  0.0 151.6 jit_solution(14008375851687026574)
XLA Ops:
  7.2 0.0 copy-start
  7.2 0.0 all-gather.3.cloned.1.call-start
  7.2 19.3 %all_gather.12 = bf16[2048,128]{1,0:T(8,128)(2,1)} all-gather(bf16[512,128]{1,0:T(8,128)(2,1)} %param.9), channel_id=1, replica_groups=mesh['gx'=8,'gy'=4] {'gy'}, dimensions={0}, use_global_device_ids=true | all-gather | bytes 655360 | tf_op jit(solution)/shard_map/all_gather | solution.py:42
  26.6 0.0 all-gather.3.cloned.1.call-update
  26.6 0.0 all-gather.5.cloned.1.call-start
  26.6 0.0 copy-start.4
  26.7 0.0 copy-start.3
  26.7 0.0 copy-start.5
  26.7 6.4 %copy.16 = bf16[32,2,256,128]{2,3,0,1:T(8,128)(2,1)} copy(bf16[32,2,256,128]{3,2,1,0:T(8,128)(2,1)} %bitcast.66) | data formatting | bytes 8388608 | tf_op jit(solution)/shard_map/reshape | solution.py:23
  33.1 0.0 copy-done.4
  33.1 0.0 copy-done.3
  33.1 0.1 select_reduce_fusion.4
  33.2 0.0 copy-done.5
  33.2 29.9 %all-gather.3.cloned.1.call-done = bf16[16384,128]{1,0:T(8,128)(2,1)} async-done(((bf16[2048,128]{1,0:T(8,128)(2,1)}), bf16[16384,128]{1,0:T(8,128)(2,1)}) %all-gather.3.cloned.1.call-update) | async-done | bytes 4194320 | tf_op jit(solution)/shard_map/all_gather | solution.py:43
  63.1 6.4 %copy.15 = bf16[32,2,256,128]{2,3,0,1:T(8,128)(2,1)} copy(bf16[32,2,256,128]{3,2,1,0:T(8,128)(2,1)} %bitcast.68) | data formatting | bytes 8388608 | tf_op jit(solution)/shard_map/reshape | solution.py:22
  69.4 0.0 copy-start.6
  69.4 4.1 %broadcast_select_fusion = bf16[32,2,256,128]{2,3,0,1:T(8,128)(2,1)S(1)} fusion(bf16[32,2,256,128]{2,3,0,1:T(8,128)(2,1)} %copy.15, bf16[32,2,256,128]{2,3,0,1:T(8,128)(2,1)} %copy.16, pred[32]{0:T(512)(128)(4,1)S(1)} %get-tuple-element.11), kind=kLoop, calls=%fused_computation.8 | loop fusion | flops 2097152 | bytes 12582944 | tf_op jit(solution)/shard_map/jit(_where)/select_n | solution.py:26
  73.6 0.5 copy-done.6
  74.1 1.6 %select_reduce_fusion.3 = (bf16[128,256]{1,0:T(8,128)(2,1)S(1)}, bf16[128,256]{1,0:T(8,128)(2,1)S(1)}) fusion(pred[32]{0:T(512)(128)(4,1)S(1)} %get-tuple-element.12, bf16[1,32,256,256]{3,2,1,0:T(8,128)(2,1)S(1)} %copy-done.6, bf16[32,2,256,128]{2,3,0,1:T(8,128)(2,1)S(1)} %broadcast_select_fusion, pred[32]{0:T(512)(128)(4,1)S(1)} %get-tuple-element.13), kind=kOutput, calls=%fused_computation.7 | convolution fusion | flops 542048256 | bytes 8519744 | tf_op jit(solution)/shard_map/kab,kbf->kaf/dot_general | solution.py:28
  75.7 0.0 copy-done
  75.7 1.8 %multiply_reduce_fusion = (f32[]{:T(128)}, bf16[512,128]{1,0:T(8,128)(2,1)S(1)}) fusion(bf16[16384,128]{1,0:T(8,128)(2,1)} %param.11, s32[]{:T(128)S(6)} %select_n.44, bf16[128,128]{1,0:T(8,128)(2,1)S(1)} %copy-done, bf16[256,128]{0,1:T(8,128)(2,1)S(1)} %bitcast.74, bf16[256,128]{0,1:T(8,128)(2,1)S(1)} %bitcast.73), kind=kOutput, calls=%fused_computation.21 | convolution fusion | flops 17498112 | bytes 425992 | tf_op jit(solution)/shard_map/dot_general | solution.py:70
  77.4 16.4 %all_gather.14 = bf16[2048,128]{1,0:T(8,128)(2,1)} all-gather(bf16[512,128]{1,0:T(8,128)(2,1)S(1)} %get-tuple-element.15), channel_id=1, replica_groups=mesh['gx'=8,'gy'=4] {'gy'}, dimensions={0}, use_global_device_ids=true | all-gather | bytes 655360 | tf_op jit(solution)/shard_map/all_gather | solution.py:42
  93.8 0.0 all-gather.5.cloned.1.call-update
  93.8 0.0 copy-start.1
  93.9 6.4 %copy.18 = bf16[32,2,256,128]{2,3,0,1:T(8,128)(2,1)} copy(bf16[32,2,256,128]{3,2,1,0:T(8,128)(2,1)} %bitcast.67) | data formatting | bytes 8388608 | tf_op jit(solution)/shard_map/reshape | solution.py:23
  100.3 0.0 copy-done.1
  100.3 1.6 %multiply_reduce_fusion.1 = f32[]{:T(128)} fusion(bf16[512,128]{1,0:T(8,128)(2,1)S(1)} %copy-done.1, bf16[16384,128]{1,0:T(8,128)(2,1)} %param.10, s32[]{:T(128)S(6)} %select_n.44), kind=kLoop, calls=%fused_computation.22 | loop fusion | flops 327679 | bytes 262152 | tf_op jit(solution)/shard_map/reduce_sum | solution.py:50
  101.9 12.9 %all-reduce = (f32[]{:T(128)}, f32[]{:T(128)}) all-reduce(f32[]{:T(128)} %get-tuple-element.14, f32[]{:T(128)} %multiply_reduce_fusion.1), channel_id=1, replica_groups=mesh['gx'=8,'gy'=4] {'gx'}, use_global_device_ids=true, to_apply=%region_9.10 | all-reduce | flops 2 | bytes 16 | tf_op jit(solution)/shard_map/psum | solution.py:54
  114.8 13.0 %all-reduce.1 = (f32[]{:T(128)}, f32[]{:T(128)}) all-reduce(f32[]{:T(128)} %get-tuple-element.6, f32[]{:T(128)} %get-tuple-element.7), channel_id=1, replica_groups=mesh['gx'=8,'gy'=4] {'gy'}, use_global_device_ids=true, to_apply=%region_10.11 | all-reduce | flops 2 | bytes 16 | tf_op jit(solution)/shard_map/psum | solution.py:54
  129.1 0.6 pad_maximum_fusion
  129.6 1.7 %all-gather.5.cloned.1.call-done = bf16[16384,128]{1,0:T(8,128)(2,1)} async-done(((bf16[2048,128]{1,0:T(8,128)(2,1)}), bf16[16384,128]{1,0:T(8,128)(2,1)}) %all-gather.5.cloned.1.call-update) | async-done | bytes 4194320 | tf_op jit(solution)/shard_map/all_gather | solution.py:43
  131.3 6.4 %copy.17 = bf16[32,2,256,128]{2,3,0,1:T(8,128)(2,1)} copy(bf16[32,2,256,128]{3,2,1,0:T(8,128)(2,1)} %bitcast.69) | data formatting | bytes 8388608 | tf_op jit(solution)/shard_map/reshape | solution.py:22
  137.7 0.0 copy-start.7
  137.7 4.1 %broadcast_select_fusion.1 = bf16[32,2,256,128]{2,3,0,1:T(8,128)(2,1)S(1)} fusion(bf16[32,2,256,128]{2,3,0,1:T(8,128)(2,1)} %copy.17, bf16[32,2,256,128]{2,3,0,1:T(8,128)(2,1)} %copy.18, pred[32]{0:T(512)(128)(4,1)S(1)} %get-tuple-element.10), kind=kLoop, calls=%fused_computation.9 | loop fusion | flops 2097152 | bytes 12582944 | tf_op jit(solution)/shard_map/jit(_where)/select_n | solution.py:26
  141.8 0.5 copy-done.7
  142.3 0.0 copy-start.2
  142.3 1.6 %select_reduce_fusion.1 = (bf16[128,256]{1,0:T(8,128)(2,1)S(1)}, bf16[128,256]{1,0:T(8,128)(2,1)S(1)}) fusion(pred[32]{0:T(512)(128)(4,1)S(1)} %get-tuple-element.12, bf16[1,32,256,256]{3,2,1,0:T(8,128)(2,1)S(1)} %copy-done.7, bf16[32,2,256,128]{2,3,0,1:T(8,128)(2,1)S(1)} %broadcast_select_fusion.1, pred[32]{0:T(512)(128)(4,1)S(1)} %get-tuple-element.13), kind=kOutput, calls=%fused_computation.5 | convolution fusion | flops 542048256 | bytes 8519744 | tf_op jit(solution)/shard_map/kab,kbf->kaf/dot_general | solution.py:28
  143.9 0.0 copy-done.2
  143.9 0.9 convolution_convert_fusion
  (3 shorter events, 0.0 us)
Async XLA Ops:
  7.2 68.5 %copy-start = (bf16[128,128]{1,0:T(8,128)(2,1)S(1)}, bf16[128,128]{1,0:T(8,128)(2,1)}, u32[]{:S(2)}) copy-start(bf16[128,128]{1,0:T(8,128)(2,1)} %param.16) | copy-start | bytes 98308
  7.2 55.9 %all-gather.3.cloned.1.call-start = ((), (), s32[]{:S(2)}) async-start(), calls=%async_computation | async-start | bytes 4718592 | tf_op jit(solution)/shard_map/all_gather | solution.py:43
  26.6 104.7 %all-gather.5.cloned.1.call-start = ((), (), s32[]{:S(2)}) async-start(), calls=%async_computation.1 | async-start | bytes 4718592 | tf_op jit(solution)/shard_map/all_gather | solution.py:43
  26.6 6.4 %copy-start.4 = (s32[2,32]{1,0:T(2,128)S(1)}, s32[2,32]{1,0:T(2,128)}, u32[]{:S(2)}) copy-start(s32[2,32]{1,0:T(2,128)} %param.15) | copy-start | bytes 772
  26.7 6.4 %copy-start.3 = (s32[2,32]{1,0:T(2,128)S(1)}, s32[2,32]{1,0:T(2,128)}, u32[]{:S(2)}) copy-start(s32[2,32]{1,0:T(2,128)} %param.14) | copy-start | bytes 772
  26.7 6.5 %copy-start.5 = (s32[1,32,2]{1,2,0:T(2,128)S(1)}, s32[1,32,2]{1,2,0:T(2,128)}, u32[]{:S(2)}) copy-start(s32[1,32,2]{1,2,0:T(2,128)} %param.13) | copy-start | bytes 772
  69.4 4.6 %copy-start.6 = (bf16[1,32,256,256]{3,2,1,0:T(8,128)(2,1)S(1)}, bf16[1,32,256,256]{3,2,1,0:T(8,128)(2,1)}, u32[]{:S(2)}) copy-start(bf16[1,32,256,256]{3,2,1,0:T(8,128)(2,1)} %param.12) | copy-start | bytes 12582916
  93.8 6.5 %copy-start.1 = (bf16[512,128]{1,0:T(8,128)(2,1)S(1)}, bf16[512,128]{1,0:T(8,128)(2,1)}, u32[]{:S(2)}) copy-start(bf16[512,128]{1,0:T(8,128)(2,1)} %param.9) | copy-start | bytes 393220
  137.7 4.6 %copy-start.7 = (bf16[1,32,256,256]{3,2,1,0:T(8,128)(2,1)S(1)}, bf16[1,32,256,256]{3,2,1,0:T(8,128)(2,1)}, u32[]{:S(2)}) copy-start(bf16[1,32,256,256]{3,2,1,0:T(8,128)(2,1)} %param.12) | copy-start | bytes 12582916
  142.3 1.6 %copy-start.2 = (bf16[128,128]{1,0:T(8,128)(2,1)S(1)}, bf16[128,128]{1,0:T(8,128)(2,1)}, u32[]{:S(2)}) copy-start(bf16[128,128]{1,0:T(8,128)(2,1)} %param.17) | copy-start | bytes 98308
Sparse Core Ops, SparseCore 0:
  26.7 36.3 all-gather.2
  94.0 37.2 all-gather.4
